TPU v7x, 32 devices: a whole 2x2x4 slice. The times are simulated.
32 devices in a mesh: vtx: 8 (over z, x), src: 4 (over y, core).
Axes of the slice: x: 2, y: 2, z: 4, core: 2. Of those that a mesh axis runs over, the one named last changes fastest.
Arguments:
- heat: float32 [64, 64, 8192], P(None, ('vtx', 'src')), may hold values from -12 to 12
- cotan: float32 [4, 64, 8192], P(None, 'vtx'), may hold values from 0.2 to 2
- source_index: int32 [64], replicated, may hold values from 0 to 524287
Outputs:
- normalised: float32 [64, 64, 8192], P('src', 'vtx')
- col_norm: float32 [64], P('src')
Inputs may be any that keep to these rules, and one draw needn't show every extreme that they name: `source_index`: row-major vertex indices, sources may share a vertex.
All inputs are finite; a program needn't handle non-finite values.
Results may differ from a plain program's by a relative error of at most 0.0003.
Values sent between devices are 32-bit elements; how exact they have to be, the bound alone decides.
A program may use at most 64 MiB of HBM per device.

v0:
```python
import math

import jax
import jax.numpy as jnp
from jax import lax
from jax.sharding import PartitionSpec as P


def from_behind(value, axis, by):
    peers = lax.axis_size(axis)
    pairs = [(i, i + by) for i in range(peers) if 0 <= i + by < peers]
    return lax.ppermute(value, axis, pairs)


def extended(value, sides, width):
    for axis, dim in sides:
        peers, length = (lax.axis_size(axis), value.shape[dim])
        up = [(i, (i + 1) % peers) for i in range(peers - 1)]
        down = [(j, i) for i, j in up]
        last = lax.slice_in_dim(value, length - width, length, axis=dim)
        first = lax.slice_in_dim(value, 0, width, axis=dim)
        before = lax.ppermute(last, axis, up)
        after = lax.ppermute(first, axis, down)
        value = jnp.concatenate([before, value, after], axis=dim)
    return value


def from_right(values):
    return jnp.concatenate([values[..., 1:], jnp.zeros_like(values[..., :1])], axis=-1)


def from_left(values):
    return jnp.concatenate([jnp.zeros_like(values[..., :1]), values[..., :-1]], axis=-1)


def masked_cotan(cotan, row_start, total_rows):
    shape = cotan.shape[1:]
    rows = row_start + lax.broadcasted_iota(jnp.int32, shape, 0)
    cols = lax.broadcasted_iota(jnp.int32, shape, 1)
    inside_col = cols < shape[1] - 1
    inside_row = rows < total_rows - 1
    mass = cotan[0]
    east = jnp.where(inside_col, cotan[1], 0.0)
    north = jnp.where(inside_row, cotan[2], 0.0)
    diag = jnp.where(inside_col & inside_row, cotan[3], 0.0)
    return (mass, east, north, diag)


def stencil_defect(padded, mass, east, north_ext, diag_ext, row_start, sources, amplitude):
    center = padded[:, 1:-1, :]
    above = padded[:, 2:, :]
    below = padded[:, :-2, :]
    north = north_ext[1:]
    south_weight = north_ext[:-1]
    diag = diag_ext[1:]
    southwest_weight = from_left(diag_ext[:-1])
    west_weight = from_left(east)
    result = mass * center + east * (center - from_right(center))
    result = result + west_weight * (center - from_left(center))
    result = result + north * (center - above) + south_weight * (center - below)
    result = (
        result
        + diag * (center - from_right(above))
        + southwest_weight * (center - from_left(below))
    )
    count_rows, width = (center.shape[1], center.shape[2])
    row_ids = row_start + lax.broadcasted_iota(jnp.int32, (count_rows, width), 0)
    col_ids = lax.broadcasted_iota(jnp.int32, (count_rows, width), 1)
    flat = row_ids * width + col_ids
    delta = (flat[None, :, :] == sources[:, None, None]).astype(jnp.float32)
    return result - amplitude * delta


def on_device(heat, cotan, source_index):
    vtx_index = lax.axis_index("vtx")
    rows_dev = cotan.shape[1]
    width = cotan.shape[2]
    total_rows = rows_dev * lax.axis_size("vtx")
    amplitude = math.sqrt(total_rows * width) / 8.0
    block_start = vtx_index * rows_dev
    mass, east, north, diag = masked_cotan(cotan, block_start, total_rows)
    lower = from_behind(jnp.stack([north[-1:], diag[-1:]]), "vtx", 1)
    north_ext = jnp.concatenate([lower[0], north], axis=0)
    diag_ext = jnp.concatenate([lower[1], diag], axis=0)
    src_index = lax.axis_index("src")
    per_group = heat.shape[0] // lax.axis_size("src")
    tile = lax.all_to_all(heat, "src", split_axis=0, concat_axis=1, tiled=True)
    padded = extended(tile, (("vtx", 1),), 1)
    sources = lax.dynamic_slice_in_dim(source_index, src_index * per_group, per_group)
    defect = stencil_defect(
        padded, mass, east, north_ext, diag_ext, block_start, sources, amplitude
    )
    total = lax.psum(jnp.sum(defect * defect, axis=(1, 2)), "vtx")
    norms = jnp.sqrt(total / (total_rows * width) + 1e-06)
    return (defect / norms[:, None, None], norms)


def solution(mesh):
    return jax.shard_map(
        on_device,
        mesh=mesh,
        in_specs=(P(None, ("vtx", "src"), None), P(None, "vtx", None), P()),
        out_specs=(P("src", "vtx", None), P("src")),
        check_vma=False,
    )
```

profile of v0, /device:TPU:0, one launch (start us, length us, event | category | flops | bytes accessed | tf_op | source)
XLA Modules:
  0.0 121.2 jit_solution(14948934049001628183)
XLA Ops:
  0.6 0.0 copy-start
  0.6 5.0 %all-to-all-start = ((f32[64,2,8192]{2,1,0:T(2,128)}), f32[64,2,8192]{2,1,0:T(2,128)}, u32[]{:S(2)}, u32[]{:S(2)}) async-start(f32[64,2,8192]{2,1,0:T(2,128)} %param.3), calls=%async_computation | async-start | bytes 8388608 | tf_op jit(solution)/shard_map/all_to_all | solution.py:87
  5.6 0.0 copy-start.2
  5.7 0.0 copy-done
  5.7 0.1 bitcast_select_fusion.1
  5.9 0.1 pad_maximum_fusion.1
  5.9 4.9 %collective-permute-start.1 = (f32[2,1,8192]{2,1,0:T(1,128)S(1)}, f32[2,1,8192]{2,1,0:T(1,128)S(1)}, u32[]{:S(2)}, u32[]{:S(2)}) collective-permute-start(f32[2,1,8192]{2,1,0:T(1,128)S(1)} %pad_maximum_fusion.1), channel_id=1, source_target_pairs={{0,4},{4,8},{8,12},{12,16},{16,20},{20,24},{24,28},{1,5},{5,9},{9,... | collective-permute-start | bytes 196616 | tf_op jit(solution)/shard_map/ppermute | solution.py:12
  10.8 0.1 slice_bitcast_fusion
  11.0 0.1 iota_add_fusion
  11.1 0.0 copy-done.2
  11.1 0.1 dynamic_slice.3
  11.2 0.1 concatenate.32
  11.3 1.4 %collective-permute-done.1 = f32[2,1,8192]{2,1,0:T(1,128)S(1)} collective-permute-done((f32[2,1,8192]{2,1,0:T(1,128)S(1)}, f32[2,1,8192]{2,1,0:T(1,128)S(1)}, u32[]{:S(2)}, u32[]{:S(2)}) %collective-permute-start.1) | collective-permute-done | bytes 65568 | tf_op jit(solution)/shard_map/ppermute | solution.py:12
  12.8 0.2 select_maximum_fusion.2
  13.0 41.6 %all-to-all-done = f32[64,2,8192]{2,1,0:T(2,128)} async-done(((f32[64,2,8192]{2,1,0:T(2,128)}), f32[64,2,8192]{2,1,0:T(2,128)}, u32[]{:S(2)}, u32[]{:S(2)}) %all-to-all-start) | async-done | bytes 4194336 | tf_op jit(solution)/shard_map/all_to_all | solution.py:87
  54.5 4.6 %copy.6 = f32[4,16,2,8192]{3,1,2,0:T(8,128)S(1)} copy(f32[4,16,2,8192]{3,2,1,0:T(2,128)} %bitcast.1) | data formatting | bytes 8388608 | tf_op jit(solution)/shard_map/all_to_all | solution.py:87
  59.2 0.1 fusion.19
  59.2 1.3 %collective-permute-start = (f32[16,1,8192]{2,0,1:T(8,128)S(1)}, f32[16,1,8192]{2,0,1:T(8,128)S(1)}, u32[]{:S(2)}, u32[]{:S(2)}) collective-permute-start(f32[16,1,8192]{2,0,1:T(8,128)S(1)} %get-tuple-element.8), channel_id=1, source_target_pairs={{4,0},{8,4},{12,8},{16,12},{20,16},{24,20},{28,24},{5,1},{9,5},{13... | collective-permute-start | bytes 1572872 | tf_op jit(solution)/shard_map/ppermute | solution.py:23
  60.5 4.8 %collective-permute-start.2 = (f32[16,1,8192]{2,0,1:T(8,128)S(1)}, f32[16,1,8192]{2,0,1:T(8,128)S(1)}, u32[]{:S(2)}, u32[]{:S(2)}) collective-permute-start(f32[16,1,8192]{2,0,1:T(8,128)S(1)} %get-tuple-element.9), channel_id=1, source_target_pairs={{0,4},{4,8},{8,12},{12,16},{16,20},{20,24},{24,28},{1,5},{5,9},{9,... | collective-permute-start | bytes 1572872 | tf_op jit(solution)/shard_map/ppermute | solution.py:22
  65.4 1.5 %fusion.18 = (f32[16,8,8191]{2,0,1:T(8,128)S(1)}, f32[16,8,8191]{2,0,1:T(8,128)S(1)}) fusion(f32[16,8,8192]{2,0,1:T(8,128)S(1)} %bitcast.28), kind=kLoop, calls=%fused_computation.47 | loop fusion | bytes 16775168 | tf_op jit(solution)/shard_map/slice | solution.py:29
  66.8 8.2 %collective-permute-done = f32[16,1,8192]{2,0,1:T(8,128)S(1)} collective-permute-done((f32[16,1,8192]{2,0,1:T(8,128)S(1)}, f32[16,1,8192]{2,0,1:T(8,128)S(1)}, u32[]{:S(2)}, u32[]{:S(2)}) %collective-permute-start) | collective-permute-done | bytes 524320 | tf_op jit(solution)/shard_map/ppermute | solution.py:23
  75.0 11.4 %collective-permute-done.2 = f32[16,1,8192]{2,0,1:T(8,128)S(1)} collective-permute-done((f32[16,1,8192]{2,0,1:T(8,128)S(1)}, f32[16,1,8192]{2,0,1:T(8,128)S(1)}, u32[]{:S(2)}, u32[]{:S(2)}) %collective-permute-start.2) | collective-permute-done | bytes 524320 | tf_op jit(solution)/shard_map/ppermute | solution.py:22
  86.4 7.7 %multiply_reduce_fusion = (f32[16]{0:T(128)S(1)}, f32[16,8,8192]{2,0,1:T(8,128)}) fusion(s32[16]{0:T(128)S(1)} %dynamic_slice.3, s32[8,8192]{1,0:T(8,128)S(1)} %iota_add_fusion, f32[16,8,8192]{2,0,1:T(8,128)S(1)} %bitcast.29, f32[16,1,8192]{2,0,1:T(8,128)S(1)} %collective-permute-done.2, f32[8,8192]{1,0:T(8,128)S(1)} %get-tuple-element.22, ...), kind=kLoop, calls=%fused_computation.23 | loop fusion | flops 35651568 | bytes 19922048 | tf_op jit(solution)/shard_map/reduce_sum | solution.py:93
  94.1 19.8 %psum.7 = f32[16]{0:T(128)S(1)} all-reduce(f32[16]{0:T(128)S(1)} %get-tuple-element.4), channel_id=1, replica_groups=mesh['vtx'=8,'src'=4] {'vtx'}, use_global_device_ids=true, to_apply=%region_1.2 | all-reduce | flops 16 | bytes 128 | tf_op jit(solution)/shard_map/psum | solution.py:93
  114.0 0.0 copy-start.1
  114.0 2.7 %broadcast_divide_fusion = f32[16,8,8192]{2,0,1:T(8,128)S(1)} fusion(f32[16,8,8192]{2,0,1:T(8,128)} %get-tuple-element.5, f32[16]{0:T(128)S(1)} %add_sqrt_fusion), kind=kLoop, calls=%fused_computation.24 | loop fusion | flops 1048576 | bytes 8388672 | tf_op jit(solution)/shard_map/div | solution.py:95
  116.7 0.0 copy-done.1
  116.7 4.4 %copy.7 = f32[16,8,8192]{2,1,0:T(8,128)} copy(f32[16,8,8192]{2,0,1:T(8,128)S(1)} %broadcast_divide_fusion) | data formatting | bytes 8388608
  (8 shorter events, 0.1 us)
Async XLA Ops:
  0.6 5.0 %copy-start = (f32[4,8,8192]{2,1,0:T(8,128)S(1)}, f32[4,8,8192]{2,1,0:T(8,128)}, u32[]{:S(2)}) copy-start(f32[4,8,8192]{2,1,0:T(8,128)} %param.4) | copy-start | bytes 3145732
  0.6 53.9 %all-to-all-start = ((f32[64,2,8192]{2,1,0:T(2,128)}), f32[64,2,8192]{2,1,0:T(2,128)}, u32[]{:S(2)}, u32[]{:S(2)}) async-start(f32[64,2,8192]{2,1,0:T(2,128)} %param.3), calls=%async_computation | async-start | bytes 8388608 | tf_op jit(solution)/shard_map/all_to_all | solution.py:87
  5.6 5.5 %copy-start.2 = (s32[64]{0:T(128)S(1)}, s32[64]{0:T(128)}, u32[]{:S(2)}) copy-start(s32[64]{0:T(128)} %param.5) | copy-start | bytes 772
  5.9 6.8 %collective-permute-start.1 = (f32[2,1,8192]{2,1,0:T(1,128)S(1)}, f32[2,1,8192]{2,1,0:T(1,128)S(1)}, u32[]{:S(2)}, u32[]{:S(2)}) collective-permute-start(f32[2,1,8192]{2,1,0:T(1,128)S(1)} %pad_maximum_fusion.1), channel_id=1, source_target_pairs={{0,4},{4,8},{8,12},{12,16},{16,20},{20,24},{24,28},{1,5},{5,9},{9,... | collective-permute-start | bytes 196616 | tf_op jit(solution)/shard_map/ppermute | solution.py:12
  59.2 15.8 %collective-permute-start = (f32[16,1,8192]{2,0,1:T(8,128)S(1)}, f32[16,1,8192]{2,0,1:T(8,128)S(1)}, u32[]{:S(2)}, u32[]{:S(2)}) collective-permute-start(f32[16,1,8192]{2,0,1:T(8,128)S(1)} %get-tuple-element.8), channel_id=1, source_target_pairs={{4,0},{8,4},{12,8},{16,12},{20,16},{24,20},{28,24},{5,1},{9,5},{13... | collective-permute-start | bytes 1572872 | tf_op jit(solution)/shard_map/ppermute | solution.py:23
  60.5 25.9 %collective-permute-start.2 = (f32[16,1,8192]{2,0,1:T(8,128)S(1)}, f32[16,1,8192]{2,0,1:T(8,128)S(1)}, u32[]{:S(2)}, u32[]{:S(2)}) collective-permute-start(f32[16,1,8192]{2,0,1:T(8,128)S(1)} %get-tuple-element.9), channel_id=1, source_target_pairs={{0,4},{4,8},{8,12},{12,16},{16,20},{20,24},{24,28},{1,5},{5,9},{9,... | collective-permute-start | bytes 1572872 | tf_op jit(solution)/shard_map/ppermute | solution.py:22
  114.0 2.7 %copy-start.1 = (f32[16]{0:T(128)}, f32[16]{0:T(128)S(1)}, u32[]{:S(2)}) copy-start(f32[16]{0:T(128)S(1)} %add_sqrt_fusion) | copy-start | bytes 196
where the time goes:
time: 122 us; the launch traced here: 121 us
  waiting for transfers between devices  62.6 us (51%)
  blocking collectives  19.8 us (16%)
  starting transfers between devices  15.9 us (13%)
  other arithmetic  11.1 us (9%)
  local copies, waits for them, and re-layouts  10.9 us (9%)
    all_to_all x1, waiting for transfers between devices, on_device(): tile = lax.all_to_all(heat, 'src', split_axis=0, concat_axis=1, tiled=True)  41.6 us
    psum x1, blocking collectives, on_device(): total = lax.psum(jnp.sum(defect * defect, axis=(1, 2)), 'vtx')  19.8 us
    ppermute x1, waiting for transfers between devices, extended(): before = lax.ppermute(last, axis, up)  11.4 us
    ppermute x1, waiting for transfers between devices, extended(): after = lax.ppermute(first, axis, down)  8.19 us
    reduce_sum x1, other arithmetic, on_device(): total = lax.psum(jnp.sum(defect * defect, axis=(1, 2)), 'vtx')  7.71 us
    all_to_all x1, starting transfers between devices, on_device(): tile = lax.all_to_all(heat, 'src', split_axis=0, concat_axis=1, tiled=True)  4.97 us
    ppermute x1, starting transfers between devices, from_behind(): return lax.ppermute(value, axis, pairs)  4.87 us
    ppermute x1, starting transfers between devices, extended(): before = lax.ppermute(last, axis, up)  4.81 us
  transfers between devices with their start and end apart: 4, of which 4 were waited for; matrix products, arithmetic and copies ran while one was open for 2% of the time, Pallas kernels for 0%

commit v1 on v0

v1 whole, which is shorter than its diff:
```python
import functools
import math

import jax
import jax.numpy as jnp
from jax import lax
from jax.experimental import pallas as pl
from jax.experimental.pallas import tpu as pltpu
from jax.sharding import PartitionSpec as P

MESH = pl.DeviceIdType.MESH
F32 = jnp.float32
LANES = 128
ROWS = 8
TILES = 16
GROUP = 2


def kernel(
    n, nv, ng, width, pitch, amplitude,
    idx_ref, heat_ref, cot_ref, out_ref, norm_ref,
    H, X, R, D, W, cot, low, sq, G,
    load_sem, cot_sem, y_send, y_recv, z_send, z_recv, p_send, p_recv,
    h_send, h_recv, w_send, w_recv, s_send, s_recv, o_sem,
):
    v = lax.axis_index("vtx")
    src = lax.axis_index("src")
    nt = width // LANES
    k0, k1 = 2, ng // GROUP
    s0 = ng // k0
    total_rows = nv * ROWS
    far = list(range(2, n))
    upper = (src * 2) // n

    def peer(j):
        return ((src // 2 + j // 2) % (n // 2)) * 2 + (src + j) % 2

    def load(j):
        at = pl.ds(peer(j) * ng, ng)
        return pltpu.make_async_copy(heat_ref.at[at], H.at[at], load_sem.at[j])

    order = far + [0, 1]
    for j in order:
        load(j).start()
    cot_load = pltpu.make_async_copy(cot_ref, cot, cot_sem)
    cot_load.start()

    barrier = pltpu.get_barrier_semaphore()
    for j in range(1, n):
        pl.semaphore_signal(barrier, inc=1, device_id={"src": peer(j)}, device_id_type=MESH)

    @pl.loop(1, nv)
    def _(o):
        pl.semaphore_signal(barrier, inc=1, device_id={"vtx": (v + o) % nv}, device_id_type=MESH)

    def extract(j):
        load(j).wait()
        base = peer(j) * ng

        @pl.loop(0, ng)
        def _(s):
            for r in range(2):
                row = H[base + s, pl.ds(r, nt, stride=2), :]
                X[r, pl.ds(pl.multiple_of((base + s) * nt, nt), nt), :] = row

    for j in far:
        extract(j)

    pl.semaphore_wait(barrier, (n - 1) + (nv - 1))

    def row_copy(r, j, first, count, send, recv):
        start = pl.multiple_of((peer(j) * ng + first) * nt, nt)
        land = pl.multiple_of((1 + 2 * src + r) * pitch + first * nt, 8)
        return pltpu.make_async_remote_copy(
            src_ref=X.at[r, pl.ds(start, count * nt)],
            dst_ref=R.at[pl.ds(land, count * nt)],
            send_sem=send, recv_sem=recv,
            device_id={"src": peer(j)}, device_id_type=MESH,
        )

    def pass0(k, j):
        return row_copy(upper, j, k * s0, s0, y_send.at[j, k], y_recv.at[j, k])

    def pass1(k, j):
        return row_copy(1 - upper, j, k * GROUP, GROUP, z_send.at[j, k], z_recv.at[j, k])

    for k in range(k0):
        for j in far:
            pass0(k, j).start()

    @pl.loop(0, k1)
    def _(k):
        for j in far:
            pass1(k, j).start()

    def weight_copy():
        return pltpu.make_async_remote_copy(
            src_ref=cot_ref.at[pl.ds(2, 2)], dst_ref=low, send_sem=w_send, recv_sem=w_recv,
            device_id={"vtx": (v + 1) % nv}, device_id_type=MESH,
        )

    @pl.when(v < nv - 1)
    def _():
        weight_copy().start()

    extract(1)

    def partner(r):
        return row_copy(r, 1, 0, ng, p_send.at[r], p_recv.at[r])

    for r in range(2):
        partner(r).start()

    load(0).wait()

    @pl.loop(0, ng)
    def _(s):
        for r in range(2):
            row = H[src * ng + s, pl.ds(r, nt, stride=2), :]
            R[pl.ds(pl.multiple_of((1 + 2 * src + r) * pitch + s * nt, 8), nt), :] = row

    @pl.when(v == 0)
    def _():
        R[pl.ds(0, ng * nt), :] = jnp.zeros((ng * nt, LANES), F32)

    @pl.when(v == nv - 1)
    def _():
        R[pl.ds(9 * pitch, ng * nt), :] = jnp.zeros((ng * nt, LANES), F32)

    def halo(up, k):
        first = k * s0 * nt
        out = (8 if up else 1) * pitch + first
        land = (0 if up else 9) * pitch + first
        to = (v + 1) % nv if up else (v + nv - 1) % nv
        return pltpu.make_async_remote_copy(
            src_ref=R.at[pl.ds(out, s0 * nt)], dst_ref=R.at[pl.ds(land, s0 * nt)],
            send_sem=h_send.at[up, k], recv_sem=h_recv.at[up, k],
            device_id={"vtx": to}, device_id_type=MESH,
        )

    def weights():
        cot_load.wait()

        @pl.when(v > 0)
        def _():
            weight_copy().wait_recv()

        shape = (ROWS, width)
        rows = lax.broadcasted_iota(jnp.int32, shape, 0)
        cols = lax.broadcasted_iota(jnp.int32, shape, 1)
        inside_col = cols < width - 1
        inside_row = rows + v * ROWS < total_rows - 1
        last = rows == ROWS - 1
        below = jnp.broadcast_to(v > 0, shape)
        W[0] = jnp.where(inside_col, cot[1], 0.0)
        W[1] = jnp.where(inside_row, cot[2], 0.0)
        W[4] = jnp.where(inside_col & inside_row, cot[3], 0.0)
        W[2] = pltpu.roll(jnp.where(last, jnp.where(below, low[0], 0.0), W[1]), 1, 0)
        W[3] = pltpu.roll(jnp.where(last, jnp.where(below & inside_col, low[1], 0.0), W[4]), 1, 0)
        W[5] = pltpu.roll(W[0], 1, 1)
        W[6] = cot[0] + W[0] + W[5] + W[1] + W[2] + W[4] + pltpu.roll(W[3], 1, 1)
        W[4] = pltpu.roll(W[4], 1, 1)

    for r in range(2):
        partner(r).wait_recv()
    weights()
    for k in range(k0):
        for j in far:
            pass0(k, j).wait_recv()

        @pl.when(v < nv - 1)
        def _():
            halo(1, k).start()

        @pl.when(v > 0)
        def _():
            halo(0, k).start()

    lane = lax.broadcasted_iota(jnp.int32, (ROWS, LANES), 1)
    flat = lax.broadcasted_iota(jnp.int32, (ROWS, LANES), 0) * width + lane
    first_lane, last_lane = lane == 0, lane == LANES - 1

    def out_copy(k):
        at = pl.ds(k * GROUP, GROUP)
        return pltpu.make_async_copy(D.at[at], out_ref.at[at], o_sem.at[k])

    def chunk(k):
        for j in far:
            pass1(k, j).wait_recv()
        spots = [
            idx_ref[src * ng + k * GROUP + i] - v * (ROWS * width) for i in range(GROUP)
        ]

        def block(b, sums):
            sums = list(sums)
            t0 = b * TILES

            def weight(m, t):
                return W[m, :, pl.ds(pl.multiple_of(t * LANES, LANES), LANES)]

            before = (t0 + nt - 1) % nt
            after = (t0 + TILES) % nt
            tiles = [t0 + i for i in range(TILES)]
            for i in range(GROUP):
                base = (k * GROUP + i) * nt

                def field(shift, t):
                    return R[pl.ds((1 + shift) * pitch + base + t, ROWS, stride=pitch), :]

                mids = [field(0, t) for t in tiles]
                ups = [field(1, t) for t in tiles]
                downs = [field(-1, t) for t in tiles]
                p = [weight(5, t) * m + weight(4, t) * u for t, m, u in zip(tiles, mids, ups)]
                q = [weight(0, t) * m + weight(3, t) * d for t, m, d in zip(tiles, mids, downs)]
                p.append(weight(5, after) * field(0, after) + weight(4, after) * field(1, after))
                q.insert(0, weight(0, before) * field(0, before) + weight(3, before) * field(-1, before))
                for c, t in enumerate(tiles):
                    right = pltpu.roll(jnp.where(first_lane, p[c + 1], p[c]), LANES - 1, 1)
                    left = pltpu.roll(jnp.where(last_lane, q[c], q[c + 1]), 1, 1)
                    d = weight(6, t) * mids[c] - weight(1, t) * ups[c] - weight(2, t) * downs[c]
                    d = d - right - left
                    d = d - jnp.where(flat == spots[i] - t * LANES, F32(amplitude), F32(0.0))
                    sums[i] = sums[i] + d * d
                    D[k * GROUP + i, :, pl.ds(pl.multiple_of(t * LANES, LANES), LANES)] = d
            return tuple(sums)

        zero = jnp.zeros((ROWS, LANES), F32)
        sums = lax.fori_loop(0, nt // TILES, block, (zero,) * GROUP)
        for i in range(GROUP):
            sq[pl.ds(k * GROUP + i, 1), :] = jnp.sum(sums[i], axis=0, keepdims=True)
        out_copy(k).start()

    per = s0 // GROUP
    for k in range(k0):
        @pl.when(v > 0)
        def _():
            halo(1, k).wait_recv()

        @pl.when(v < nv - 1)
        def _():
            halo(0, k).wait_recv()

        @pl.loop(k * per, (k + 1) * per)
        def _(c):
            chunk(c)

    def share(to, slot):
        return pltpu.make_async_remote_copy(
            src_ref=sq, dst_ref=G.at[slot], send_sem=s_send.at[to], recv_sem=s_recv.at[slot],
            device_id={"vtx": to}, device_id_type=MESH,
        )

    @pl.loop(1, nv)
    def _(o):
        share((v + o) % nv, v).start()

    G[v] = sq[...]
    for j in far:
        for k in range(k0):
            pass0(k, j).wait_send()

        @pl.loop(0, k1)
        def _(k):
            pass1(k, j).wait_send()
    for r in range(2):
        partner(r).wait_send()

    @pl.when(v < nv - 1)
    def _():
        weight_copy().wait_send()
        for k in range(k0):
            halo(1, k).wait_send()

    @pl.when(v > 0)
    def _():
        for k in range(k0):
            halo(0, k).wait_send()

    @pl.loop(0, k1)
    def _(k):
        out_copy(k).wait()

    @pl.loop(1, nv)
    def _(o):
        share((v + o) % nv, (v + o) % nv).wait_recv()

    total = lax.fori_loop(0, nv, lambda i, t: t + G[i], jnp.zeros((ng, LANES), F32))
    total = jnp.sum(total, axis=1, keepdims=True)
    norms = jnp.sqrt(total / (total_rows * width) + 1e-06)
    norm_ref[...] = jnp.broadcast_to(norms, (ng, LANES))

    @pl.loop(1, nv)
    def _(o):
        share((v + o) % nv, v).wait_send()


def on_device(n, nv, heat, cotan, source_index):
    sources, rpd, width = heat.shape
    assert rpd == 2 and cotan.shape[1] == ROWS and n % 2 == 0
    ng = sources // n
    nt = width // LANES
    pitch = -(-(ng * nt) // 64) * 64 + 8
    amplitude = math.sqrt(ROWS * nv * width) / 8.0
    tiled = heat.reshape(sources, rpd, nt, LANES).transpose(0, 2, 1, 3)
    tiled = tiled.reshape(sources, rpd * nt, LANES)
    dma = pltpu.SemaphoreType.DMA
    k0, k1 = 2, ng // GROUP
    defect, norms = pl.pallas_call(
        functools.partial(kernel, n, nv, ng, width, pitch, amplitude),
        out_shape=(
            jax.ShapeDtypeStruct((ng, ROWS, width), F32),
            jax.ShapeDtypeStruct((ng, LANES), F32),
        ),
        in_specs=[
            pl.BlockSpec(memory_space=pltpu.SMEM),
            pl.BlockSpec(memory_space=pl.ANY),
            pl.BlockSpec(memory_space=pl.ANY),
        ],
        out_specs=(
            pl.BlockSpec(memory_space=pl.ANY),
            pl.BlockSpec(memory_space=pltpu.VMEM),
        ),
        scratch_shapes=[
            pltpu.VMEM((sources, rpd * nt, LANES), F32),
            pltpu.VMEM((rpd, sources * nt, LANES), F32),
            pltpu.VMEM((10 * pitch, LANES), F32),
            pltpu.VMEM((ng, ROWS, width), F32),
            pltpu.VMEM((7, ROWS, width), F32),
            pltpu.VMEM((4, ROWS, width), F32),
            pltpu.VMEM((2, ROWS, width), F32),
            pltpu.VMEM((ng, LANES), F32),
            pltpu.VMEM((nv, ng, LANES), F32),
            dma((n,)), dma,
            dma((n, k0)), dma((n, k0)), dma((n, k1)), dma((n, k1)),
            dma((2,)), dma((2,)), dma((2, k0)), dma((2, k0)),
            dma, dma, dma((nv,)), dma((nv,)), dma((k1,)),
        ],
        compiler_params=pltpu.CompilerParams(collective_id=0, has_side_effects=True),
    )(source_index, tiled, cotan)
    norms = norms[:, 0]
    return (defect / norms[:, None, None], norms)


def solution(mesh):
    n, nv = mesh.shape["src"], mesh.shape["vtx"]
    return jax.shard_map(
        functools.partial(on_device, n, nv),
        mesh=mesh,
        in_specs=(P(None, ("vtx", "src"), None), P(None, "vtx", None), P()),
        out_specs=(P("src", "vtx", None), P("src")),
        check_vma=False,
    )
```

time: 122 us -> 66 us (0.54)
  waiting for transfers between devices: 62.6 us -> 0 us
  Pallas kernels: 0 us -> 59.6 us
  blocking collectives: 19.8 us -> 0 us
  starting transfers between devices: 15.9 us -> 0 us
  local copies, waits for them, and re-layouts: 10.9 us -> 0.81 us
  other arithmetic: 11.1 us -> 4.67 us
    pallas_call x0 -> x1, Pallas kernels: none -> 59.6 us  [on_device(): pl.pallas_call(functools.partial(kernel, n, nv, ng, width, pitch, amplitu...]
    all_to_all x1 -> x0, waiting for transfers between devices: 41.6 us -> none  [on_device(): tile = lax.all_to_all(heat, 'src', split_axis=0, concat_axis=1, tiled=True)]
    ppermute x3 -> x0, waiting for transfers between devices: 21 us -> none  [the longest x1 11.4 us: extended(): before = lax.ppermute(last, axis, up)]
    psum x1 -> x0, blocking collectives: 19.8 us -> none  [on_device(): total = lax.psum(jnp.sum(defect * defect, axis=(1, 2)), 'vtx')]
    ppermute x3 -> x0, starting transfers between devices: 11 us -> none  [the longest x1 4.87 us: from_behind(): return lax.ppermute(value, axis, pairs)]
    reduce_sum x1 -> x0, other arithmetic: 7.71 us -> none  [on_device(): total = lax.psum(jnp.sum(defect * defect, axis=(1, 2)), 'vtx')]
    all_to_all x1 -> x0, starting transfers between devices: 4.97 us -> none  [on_device(): tile = lax.all_to_all(heat, 'src', split_axis=0, concat_axis=1, tiled=True)]
    all_to_all x1 -> x0, local copies, waits for them, and re-layouts: 4.62 us -> none  [on_device(): tile = lax.all_to_all(heat, 'src', split_axis=0, concat_axis=1, tiled=True)]
  transfers between devices with their start and end apart: 4 -> 0, of which waited for: 4 -> 0; matrix products, arithmetic and copies ran while one was open for 2% -> 0% of each run, Pallas kernels for 0% -> 0%
where the time goes in v1:
time: 66 us; the launch traced here: 65.8 us
  Pallas kernels  59.6 us (90%)
  other arithmetic  4.67 us (7%)
  local copies, waits for them, and re-layouts  0.81 us (1%)
    pallas_call x1, Pallas kernels, on_device(): pl.pallas_call(functools.partial(kernel, n, nv, ng, width, pitch, amplitu...  59.6 us
    div x1, other arithmetic, on_device(): return (defect / norms[:, None, None], norms)  4.67 us

profile of v1, /device:TPU:0, one launch (start us, length us, event | category | flops | bytes accessed | tf_op | source)
XLA Modules:
  0.0 65.8 jit_solution(18196845099187200030)
XLA Ops:
  0.6 59.6 %shard_map.50 = (f32[16,8,8192]{2,1,0:T(8,128)}, f32[16,128]{1,0:T(8,128)}) custom-call(s32[64]{0:T(128)} %idx_ref.1, f32[64,128,128]{2,1,0:T(8,128)} %bitcast.5, f32[4,8,8192]{2,1,0:T(8,128)} %cot_ref.1), custom_call_target="tpu_custom_call" | custom-call | tf_op jit(solution)/shard_map/pallas_call | solution.py:308
  60.3 0.8 %slice_reduce_fusion = f32[16]{0:T(128)S(1)} fusion(f32[16,128]{1,0:T(8,128)} %get-tuple-element.5), kind=kLoop, calls=%fused_computation.1 | loop fusion | bytes 128 | tf_op jit(solution)/shard_map/slice | solution.py:340
  61.1 0.0 copy-start
  61.1 4.7 %broadcast_divide_fusion = f32[16,8,8192]{2,1,0:T(8,128)} fusion(f32[16,8,8192]{2,1,0:T(8,128)} %get-tuple-element.4, f32[16]{0:T(128)S(1)} %slice_reduce_fusion), kind=kLoop, calls=%fused_computation | loop fusion | flops 1048576 | bytes 8388672 | tf_op jit(solution)/shard_map/div | solution.py:341
  65.8 0.0 copy-done
Async XLA Ops:
  61.1 4.7 %copy-start = (f32[16]{0:T(128)}, f32[16]{0:T(128)S(1)}, u32[]{:S(2)}) copy-start(f32[16]{0:T(128)S(1)} %slice_reduce_fusion) | copy-start | bytes 196

commit v2 on v1

--- a/solution.py
+++ b/solution.py
@@ -12,21 +12,21 @@
 F32 = jnp.float32
 LANES = 128
 ROWS = 8
-TILES = 16
+BLOCK = 32
 GROUP = 2
 
 
 def kernel(
     n, nv, ng, width, pitch, amplitude,
-    idx_ref, heat_ref, cot_ref, out_ref, norm_ref,
-    H, X, R, D, W, cot, low, sq, G,
-    load_sem, cot_sem, y_send, y_recv, z_send, z_recv, p_send, p_recv,
-    h_send, h_recv, w_send, w_recv, s_send, s_recv, o_sem,
+    idx_hbm, heat_ref, cot_ref, D, norm_ref,
+    idx_ref, H, X, R, W, cot, low, sq, G,
+    idx_sem, load_sem, cot_sem, y_send, y_recv, z_send, z_recv, p_send, p_recv,
+    h_send, h_recv, w_send, w_recv, s_send, s_recv,
 ):
     v = lax.axis_index("vtx")
     src = lax.axis_index("src")
     nt = width // LANES
-    k0, k1 = 2, ng // GROUP
+    k0, k1 = 2, ng // GROUP + 1
     s0 = ng // k0
     total_rows = nv * ROWS
     far = list(range(2, n))
@@ -35,15 +35,18 @@
     def peer(j):
         return ((src // 2 + j // 2) % (n // 2)) * 2 + (src + j) % 2
 
-    def load(j):
-        at = pl.ds(peer(j) * ng, ng)
-        return pltpu.make_async_copy(heat_ref.at[at], H.at[at], load_sem.at[j])
-
-    order = far + [0, 1]
-    for j in order:
-        load(j).start()
+    def load(j, k):
+        at = pl.ds(peer(j) * ng + k * s0, s0)
+        return pltpu.make_async_copy(heat_ref.at[at], H.at[at], load_sem.at[j, k])
+
+    for j_set in (far, [1, 0]):
+        for k in range(k0):
+            for j in j_set:
+                load(j, k).start()
     cot_load = pltpu.make_async_copy(cot_ref, cot, cot_sem)
     cot_load.start()
+    idx_load = pltpu.make_async_copy(idx_hbm, idx_ref, idx_sem)
+    idx_load.start()
 
     barrier = pltpu.get_barrier_semaphore()
     for j in range(1, n):
@@ -53,20 +56,11 @@
     def _(o):
         pl.semaphore_signal(barrier, inc=1, device_id={"vtx": (v + o) % nv}, device_id_type=MESH)
 
-    def extract(j):
-        load(j).wait()
-        base = peer(j) * ng
-
-        @pl.loop(0, ng)
-        def _(s):
-            for r in range(2):
-                row = H[base + s, pl.ds(r, nt, stride=2), :]
-                X[r, pl.ds(pl.multiple_of((base + s) * nt, nt), nt), :] = row
-
-    for j in far:
-        extract(j)
-
-    pl.semaphore_wait(barrier, (n - 1) + (nv - 1))
+    def extract(first, count, r):
+        @pl.loop(0, count, unroll=4)
+        def _(i):
+            row = H[first + i, pl.ds(r, nt, stride=2), :]
+            X[r, pl.ds(pl.multiple_of((first + i) * nt, nt), nt), :] = row
 
     def row_copy(r, j, first, count, send, recv):
         start = pl.multiple_of((peer(j) * ng + first) * nt, nt)
@@ -81,17 +75,33 @@
     def pass0(k, j):
         return row_copy(upper, j, k * s0, s0, y_send.at[j, k], y_recv.at[j, k])
 
-    def pass1(k, j):
-        return row_copy(1 - upper, j, k * GROUP, GROUP, z_send.at[j, k], z_recv.at[j, k])
-
-    for k in range(k0):
-        for j in far:
+    def pass1(k, j, first, count):
+        return row_copy(1 - upper, j, first, count, z_send.at[j, k], z_recv.at[j, k])
+
+    for k in range(k0):
+        for j in far:
+            load(j, k).wait()
+            extract(peer(j) * ng + k * s0, s0, upper)
+            if k == 0 and j == far[0]:
+                pl.semaphore_wait(barrier, (n - 1) + (nv - 1))
             pass0(k, j).start()
 
-    @pl.loop(0, k1)
-    def _(k):
-        for j in far:
-            pass1(k, j).start()
+    for j in far:
+        extract(peer(j) * ng, ng, 1 - upper)
+
+    def each_chunk(low, high, body):
+        @pl.loop(low, min(high, k1 - 2))
+        def _(k):
+            body(k, k * GROUP, GROUP)
+
+        for k in range(k1 - 2, high):
+            body(k, ng - k1 + k, 1)
+
+    def start_pass1(k, first, count):
+        for j in far:
+            pass1(k, j, first, count).start()
+
+    each_chunk(0, k1, start_pass1)
 
     def weight_copy():
         return pltpu.make_async_remote_copy(
@@ -103,7 +113,10 @@
     def _():
         weight_copy().start()
 
-    extract(1)
+    for k in range(k0):
+        load(1, k).wait()
+    for r in range(2):
+        extract(peer(1) * ng, ng, r)
 
     def partner(r):
         return row_copy(r, 1, 0, ng, p_send.at[r], p_recv.at[r])
@@ -111,7 +124,8 @@
     for r in range(2):
         partner(r).start()
 
-    load(0).wait()
+    for k in range(k0):
+        load(0, k).wait()
 
     @pl.loop(0, ng)
     def _(s):
@@ -140,6 +154,7 @@
 
     def weights():
         cot_load.wait()
+        idx_load.wait()
 
         @pl.when(v > 0)
         def _():
@@ -180,29 +195,24 @@
     flat = lax.broadcasted_iota(jnp.int32, (ROWS, LANES), 0) * width + lane
     first_lane, last_lane = lane == 0, lane == LANES - 1
 
-    def out_copy(k):
-        at = pl.ds(k * GROUP, GROUP)
-        return pltpu.make_async_copy(D.at[at], out_ref.at[at], o_sem.at[k])
-
-    def chunk(k):
-        for j in far:
-            pass1(k, j).wait_recv()
-        spots = [
-            idx_ref[src * ng + k * GROUP + i] - v * (ROWS * width) for i in range(GROUP)
-        ]
+    def chunk(k, first, count):
+        tiles_per = BLOCK // count
+        for j in far:
+            pass1(k, j, first, count).wait_recv()
+        spots = [idx_ref[src * ng + first + i] - v * (ROWS * width) for i in range(count)]
 
         def block(b, sums):
             sums = list(sums)
-            t0 = b * TILES
+            t0 = b * tiles_per
 
             def weight(m, t):
                 return W[m, :, pl.ds(pl.multiple_of(t * LANES, LANES), LANES)]
 
             before = (t0 + nt - 1) % nt
-            after = (t0 + TILES) % nt
-            tiles = [t0 + i for i in range(TILES)]
-            for i in range(GROUP):
-                base = (k * GROUP + i) * nt
+            after = (t0 + tiles_per) % nt
+            tiles = [t0 + i for i in range(tiles_per)]
+            for i in range(count):
+                base = (first + i) * nt
 
                 def field(shift, t):
                     return R[pl.ds((1 + shift) * pitch + base + t, ROWS, stride=pitch), :]
@@ -221,16 +231,15 @@
                     d = d - right - left
                     d = d - jnp.where(flat == spots[i] - t * LANES, F32(amplitude), F32(0.0))
                     sums[i] = sums[i] + d * d
-                    D[k * GROUP + i, :, pl.ds(pl.multiple_of(t * LANES, LANES), LANES)] = d
+                    D[first + i, :, pl.ds(pl.multiple_of(t * LANES, LANES), LANES)] = d
             return tuple(sums)
 
         zero = jnp.zeros((ROWS, LANES), F32)
-        sums = lax.fori_loop(0, nt // TILES, block, (zero,) * GROUP)
-        for i in range(GROUP):
-            sq[pl.ds(k * GROUP + i, 1), :] = jnp.sum(sums[i], axis=0, keepdims=True)
-        out_copy(k).start()
-
-    per = s0 // GROUP
+        sums = lax.fori_loop(0, nt // tiles_per, block, (zero,) * count)
+        for i in range(count):
+            sq[pl.ds(first + i, 1), :] = jnp.sum(sums[i], axis=0, keepdims=True)
+
+    cuts = [0, s0 // GROUP, k1]
     for k in range(k0):
         @pl.when(v > 0)
         def _():
@@ -240,9 +249,7 @@
         def _():
             halo(0, k).wait_recv()
 
-        @pl.loop(k * per, (k + 1) * per)
-        def _(c):
-            chunk(c)
+        each_chunk(cuts[k], cuts[k + 1], chunk)
 
     def share(to, slot):
         return pltpu.make_async_remote_copy(
@@ -259,9 +266,11 @@
         for k in range(k0):
             pass0(k, j).wait_send()
 
-        @pl.loop(0, k1)
-        def _(k):
-            pass1(k, j).wait_send()
+    def end_pass1(k, first, count):
+        for j in far:
+            pass1(k, j, first, count).wait_send()
+
+    each_chunk(0, k1, end_pass1)
     for r in range(2):
         partner(r).wait_send()
 
@@ -275,10 +284,6 @@
     def _():
         for k in range(k0):
             halo(0, k).wait_send()
-
-    @pl.loop(0, k1)
-    def _(k):
-        out_copy(k).wait()
 
     @pl.loop(1, nv)
     def _(o):
@@ -292,6 +297,28 @@
     @pl.loop(1, nv)
     def _(o):
         share((v + o) % nv, v).wait_send()
+
+
+def scale(ng, nt, d_ref, n_ref, out_ref, norm_ref, O, sem):
+    lane = lax.broadcasted_iota(jnp.int32, (ng, ng), 1)
+    row = lax.broadcasted_iota(jnp.int32, (ng, ng), 0)
+
+    def put(s):
+        return pltpu.make_async_copy(O.at[s], out_ref.at[s], sem.at[s])
+
+    @pl.loop(0, ng)
+    def _(s):
+        factor = jnp.broadcast_to(1.0 / n_ref[pl.ds(s, 1), :], (ROWS, LANES))
+        for t in range(nt):
+            at = pl.ds(t * LANES, LANES)
+            O[s, :, at] = d_ref[s, :, at] * factor
+        put(s).start()
+
+    norm_ref[...] = jnp.sum(jnp.where(lane == row, n_ref[:, :ng], 0.0), axis=0, keepdims=True)
+
+    @pl.loop(0, ng)
+    def _(s):
+        put(s).wait()
 
 
 def on_device(n, nv, heat, cotan, source_index):
@@ -304,7 +331,7 @@
     tiled = heat.reshape(sources, rpd, nt, LANES).transpose(0, 2, 1, 3)
     tiled = tiled.reshape(sources, rpd * nt, LANES)
     dma = pltpu.SemaphoreType.DMA
-    k0, k1 = 2, ng // GROUP
+    k0, k1 = 2, ng // GROUP + 1
     defect, norms = pl.pallas_call(
         functools.partial(kernel, n, nv, ng, width, pitch, amplitude),
         out_shape=(
@@ -312,33 +339,48 @@
             jax.ShapeDtypeStruct((ng, LANES), F32),
         ),
         in_specs=[
-            pl.BlockSpec(memory_space=pltpu.SMEM),
-            pl.BlockSpec(memory_space=pl.ANY),
-            pl.BlockSpec(memory_space=pl.ANY),
+            pl.BlockSpec(memory_space=pltpu.HBM),
+            pl.BlockSpec(memory_space=pltpu.HBM),
+            pl.BlockSpec(memory_space=pltpu.HBM),
         ],
         out_specs=(
-            pl.BlockSpec(memory_space=pl.ANY),
             pl.BlockSpec(memory_space=pltpu.VMEM),
+            pl.BlockSpec(memory_space=pltpu.VMEM),
         ),
         scratch_shapes=[
+            pltpu.SMEM((sources,), jnp.int32),
             pltpu.VMEM((sources, rpd * nt, LANES), F32),
             pltpu.VMEM((rpd, sources * nt, LANES), F32),
             pltpu.VMEM((10 * pitch, LANES), F32),
-            pltpu.VMEM((ng, ROWS, width), F32),
             pltpu.VMEM((7, ROWS, width), F32),
             pltpu.VMEM((4, ROWS, width), F32),
             pltpu.VMEM((2, ROWS, width), F32),
             pltpu.VMEM((ng, LANES), F32),
             pltpu.VMEM((nv, ng, LANES), F32),
-            dma((n,)), dma,
+            dma, dma((n, k0)), dma,
             dma((n, k0)), dma((n, k0)), dma((n, k1)), dma((n, k1)),
             dma((2,)), dma((2,)), dma((2, k0)), dma((2, k0)),
-            dma, dma, dma((nv,)), dma((nv,)), dma((k1,)),
+            dma, dma, dma((nv,)), dma((nv,)),
         ],
-        compiler_params=pltpu.CompilerParams(collective_id=0, has_side_effects=True),
-    )(source_index, tiled, cotan)
-    norms = norms[:, 0]
-    return (defect / norms[:, None, None], norms)
+        compiler_params=pltpu.CompilerParams(
+            collective_id=0, has_side_effects=True, vmem_limit_bytes=24 * 2**20
+        ),
+    )(*(pltpu.with_memory_space_constraint(x, pltpu.HBM) for x in (source_index, tiled, cotan)))
+    out, norms = pl.pallas_call(
+        functools.partial(scale, ng, nt),
+        out_shape=(
+            jax.ShapeDtypeStruct((ng, ROWS, width), F32),
+            jax.ShapeDtypeStruct((1, ng), F32),
+        ),
+        in_specs=[pl.BlockSpec(memory_space=pltpu.VMEM)] * 2,
+        out_specs=(
+            pl.BlockSpec(memory_space=pltpu.HBM),
+            pl.BlockSpec(memory_space=pltpu.VMEM),
+        ),
+        scratch_shapes=[pltpu.VMEM((ng, ROWS, width), F32), dma((ng,))],
+        compiler_params=pltpu.CompilerParams(vmem_limit_bytes=16 * 2**20),
+    )(defect, norms)
+    return (out, norms.reshape(ng))
 
 
 def solution(mesh):

time: 66 us -> 60.7 us (0.920)
  other arithmetic: 4.67 us -> 0 us
  local copies, waits for them, and re-layouts: 0.81 us -> 0 us
    div x1 -> x0, other arithmetic: 4.67 us -> none  [on_device(): return (defect / norms[:, None, None], norms)]
    pallas_call x0 -> x1, Pallas kernels: none -> 2.67 us  [on_device(): pl.pallas_call(functools.partial(scale, ng, nt), out_shape=(jax.ShapeDtyp...]
    pallas_call x1, Pallas kernels: 59.6 us -> 57.3 us  [on_device(): pl.pallas_call(functools.partial(kernel, n, nv, ng, width, pitch, amplitu...]
    slice x1 -> x0, local copies, waits for them, and re-layouts: 0.81 us -> none  [on_device(): norms = norms[:, 0]]
where the time goes in v2:
time: 60.7 us; the launch traced here: 60.6 us
  Pallas kernels  60 us (99%)
  between operations  0.64 us (1%)
    pallas_call x1, Pallas kernels, on_device(): pl.pallas_call(functools.partial(kernel, n, nv, ng, width, pitch, amplitu...  57.3 us
    pallas_call x1, Pallas kernels, on_device(): pl.pallas_call(functools.partial(scale, ng, nt), out_shape=(jax.ShapeDtyp...  2.67 us

profile of v2, /device:TPU:0, one launch (start us, length us, event | category | flops | bytes accessed | tf_op | source)
XLA Modules:
  0.0 60.6 jit_solution(2205287449724289278)
XLA Ops:
  0.6 57.3 %shard_map.50 = (f32[16,8,8192]{2,1,0:T(8,128)S(1)}, f32[16,128]{1,0:T(8,128)S(1)}) custom-call(s32[64]{0:T(128)} %idx_hbm.1, f32[64,128,128]{2,1,0:T(8,128)} %bitcast.6, f32[4,8,8192]{2,1,0:T(8,128)} %cot_ref.1), custom_call_target="tpu_custom_call" | custom-call | tf_op jit(solution)/shard_map/pallas_call | solution.py:335
  57.9 2.7 %shard_map.51 = (f32[16,8,8192]{2,1,0:T(8,128)}, f32[1,16]{1,0:T(1,128)}) custom-call(f32[16,8,8192]{2,1,0:T(8,128)S(1)} %get-tuple-element.6.d_ref, f32[16,128]{1,0:T(8,128)S(1)} %get-tuple-element.7.n_ref), custom_call_target="tpu_custom_call" | custom-call | tf_op jit(solution)/shard_map/pallas_call | solution.py:369

commit v3 on v2

--- a/solution.py
+++ b/solution.py
@@ -9,6 +9,7 @@
 from jax.sharding import PartitionSpec as P
 
 MESH = pl.DeviceIdType.MESH
+CUTS = 4
 F32 = jnp.float32
 LANES = 128
 ROWS = 8
@@ -19,14 +20,14 @@
 def kernel(
     n, nv, ng, width, pitch, amplitude,
     idx_hbm, heat_ref, cot_ref, D, norm_ref,
-    idx_ref, H, X, R, W, cot, low, sq, G,
+    idx_ref, H, X, R, W, cot, low, sq, packed, G,
     idx_sem, load_sem, cot_sem, y_send, y_recv, z_send, z_recv, p_send, p_recv,
     h_send, h_recv, w_send, w_recv, s_send, s_recv,
 ):
     v = lax.axis_index("vtx")
     src = lax.axis_index("src")
     nt = width // LANES
-    k0, k1 = 2, ng // GROUP + 1
+    k0, k1 = CUTS, ng // GROUP + 1
     s0 = ng // k0
     total_rows = nv * ROWS
     far = list(range(2, n))
@@ -39,15 +40,8 @@
         at = pl.ds(peer(j) * ng + k * s0, s0)
         return pltpu.make_async_copy(heat_ref.at[at], H.at[at], load_sem.at[j, k])
 
-    for j_set in (far, [1, 0]):
-        for k in range(k0):
-            for j in j_set:
-                load(j, k).start()
-    cot_load = pltpu.make_async_copy(cot_ref, cot, cot_sem)
-    cot_load.start()
-    idx_load = pltpu.make_async_copy(idx_hbm, idx_ref, idx_sem)
-    idx_load.start()
-
+    for j in far:
+        load(j, 0).start()
     barrier = pltpu.get_barrier_semaphore()
     for j in range(1, n):
         pl.semaphore_signal(barrier, inc=1, device_id={"src": peer(j)}, device_id_type=MESH)
@@ -78,9 +72,22 @@
     def pass1(k, j, first, count):
         return row_copy(1 - upper, j, first, count, z_send.at[j, k], z_recv.at[j, k])
 
+    load(far[0], 0).wait()
+    for k in range(1, k0):
+        for j in far:
+            load(j, k).start()
+    for j in (1, 0):
+        for k in range(k0):
+            load(j, k).start()
+    cot_load = pltpu.make_async_copy(cot_ref, cot, cot_sem)
+    cot_load.start()
+    idx_load = pltpu.make_async_copy(idx_hbm, idx_ref, idx_sem)
+    idx_load.start()
+
     for k in range(k0):
         for j in far:
-            load(j, k).wait()
+            if k > 0 or j != far[0]:
+                load(j, k).wait()
             extract(peer(j) * ng + k * s0, s0, upper)
             if k == 0 and j == far[0]:
                 pl.semaphore_wait(barrier, (n - 1) + (nv - 1))
@@ -239,7 +246,7 @@
         for i in range(count):
             sq[pl.ds(first + i, 1), :] = jnp.sum(sums[i], axis=0, keepdims=True)
 
-    cuts = [0, s0 // GROUP, k1]
+    cuts = [k * s0 // GROUP for k in range(k0)] + [k1]
     for k in range(k0):
         @pl.when(v > 0)
         def _():
@@ -253,15 +260,21 @@
 
     def share(to, slot):
         return pltpu.make_async_remote_copy(
-            src_ref=sq, dst_ref=G.at[slot], send_sem=s_send.at[to], recv_sem=s_recv.at[slot],
+            src_ref=packed, dst_ref=G.at[slot], send_sem=s_send.at[to], recv_sem=s_recv.at[slot],
             device_id={"vtx": to}, device_id_type=MESH,
         )
+
+    spot = lax.broadcasted_iota(jnp.int32, (ng, LANES), 1)
+    on_spot = spot == lax.broadcasted_iota(jnp.int32, (ng, LANES), 0)
+    totals = jnp.sum(sq[...], axis=1, keepdims=True)
+    mine = jnp.sum(jnp.where(on_spot, totals, 0.0), axis=0, keepdims=True)
+    packed[...] = mine
 
     @pl.loop(1, nv)
     def _(o):
         share((v + o) % nv, v).start()
 
-    G[v] = sq[...]
+    G[v] = mine
     for j in far:
         for k in range(k0):
             pass0(k, j).wait_send()
@@ -289,33 +302,32 @@
     def _(o):
         share((v + o) % nv, (v + o) % nv).wait_recv()
 
-    total = lax.fori_loop(0, nv, lambda i, t: t + G[i], jnp.zeros((ng, LANES), F32))
-    total = jnp.sum(total, axis=1, keepdims=True)
-    norms = jnp.sqrt(total / (total_rows * width) + 1e-06)
-    norm_ref[...] = jnp.broadcast_to(norms, (ng, LANES))
+    total = lax.fori_loop(0, nv, lambda i, t: t + G[i], jnp.zeros((1, LANES), F32))
+    norm_ref[...] = jnp.sqrt(total / (total_rows * width) + 1e-06)
 
     @pl.loop(1, nv)
     def _(o):
         share((v + o) % nv, v).wait_send()
 
 
-def scale(ng, nt, d_ref, n_ref, out_ref, norm_ref, O, sem):
-    lane = lax.broadcasted_iota(jnp.int32, (ng, ng), 1)
-    row = lax.broadcasted_iota(jnp.int32, (ng, ng), 0)
+def scale(ng, nt, d_ref, n_ref, out_ref, norm_ref, F, O, sem):
+    lane = lax.broadcasted_iota(jnp.int32, (ng, LANES), 1)
+    row = lax.broadcasted_iota(jnp.int32, (ng, LANES), 0)
+    inverse = jnp.sum(jnp.where(lane == row, 1.0 / n_ref[...], 0.0), axis=1, keepdims=True)
+    F[...] = jnp.broadcast_to(inverse, (ng, LANES))
+    norm_ref[...] = n_ref[:, :ng]
 
     def put(s):
         return pltpu.make_async_copy(O.at[s], out_ref.at[s], sem.at[s])
 
     @pl.loop(0, ng)
     def _(s):
-        factor = jnp.broadcast_to(1.0 / n_ref[pl.ds(s, 1), :], (ROWS, LANES))
+        factor = jnp.broadcast_to(F[pl.ds(s, 1), :], (ROWS, LANES))
         for t in range(nt):
             at = pl.ds(t * LANES, LANES)
             O[s, :, at] = d_ref[s, :, at] * factor
         put(s).start()
 
-    norm_ref[...] = jnp.sum(jnp.where(lane == row, n_ref[:, :ng], 0.0), axis=0, keepdims=True)
-
     @pl.loop(0, ng)
     def _(s):
         put(s).wait()
@@ -325,18 +337,19 @@
     sources, rpd, width = heat.shape
     assert rpd == 2 and cotan.shape[1] == ROWS and n % 2 == 0
     ng = sources // n
+    assert ng <= LANES and ng % (CUTS * GROUP) == 0
     nt = width // LANES
     pitch = -(-(ng * nt) // 64) * 64 + 8
     amplitude = math.sqrt(ROWS * nv * width) / 8.0
     tiled = heat.reshape(sources, rpd, nt, LANES).transpose(0, 2, 1, 3)
     tiled = tiled.reshape(sources, rpd * nt, LANES)
     dma = pltpu.SemaphoreType.DMA
-    k0, k1 = 2, ng // GROUP + 1
+    k0, k1 = CUTS, ng // GROUP + 1
     defect, norms = pl.pallas_call(
         functools.partial(kernel, n, nv, ng, width, pitch, amplitude),
         out_shape=(
             jax.ShapeDtypeStruct((ng, ROWS, width), F32),
-            jax.ShapeDtypeStruct((ng, LANES), F32),
+            jax.ShapeDtypeStruct((1, LANES), F32),
         ),
         in_specs=[
             pl.BlockSpec(memory_space=pltpu.HBM),
@@ -356,7 +369,8 @@
             pltpu.VMEM((4, ROWS, width), F32),
             pltpu.VMEM((2, ROWS, width), F32),
             pltpu.VMEM((ng, LANES), F32),
-            pltpu.VMEM((nv, ng, LANES), F32),
+            pltpu.VMEM((1, LANES), F32),
+            pltpu.VMEM((nv, 1, LANES), F32),
             dma, dma((n, k0)), dma,
             dma((n, k0)), dma((n, k0)), dma((n, k1)), dma((n, k1)),
             dma((2,)), dma((2,)), dma((2, k0)), dma((2, k0)),
@@ -377,7 +391,9 @@
             pl.BlockSpec(memory_space=pltpu.HBM),
             pl.BlockSpec(memory_space=pltpu.VMEM),
         ),
-        scratch_shapes=[pltpu.VMEM((ng, ROWS, width), F32), dma((ng,))],
+        scratch_shapes=[
+            pltpu.VMEM((ng, LANES), F32), pltpu.VMEM((ng, ROWS, width), F32), dma((ng,))
+        ],
         compiler_params=pltpu.CompilerParams(vmem_limit_bytes=16 * 2**20),
     )(defect, norms)
     return (out, norms.reshape(ng))

time: 60.7 us -> 61 us (level)
  no operation moved by 1% of the time
where the time goes in v3:
time: 61 us; the launch traced here: 60.8 us
  Pallas kernels  60.2 us (99%)
  between operations  0.64 us (1%)
    pallas_call x1, Pallas kernels, on_device(): pl.pallas_call(functools.partial(kernel, n, nv, ng, width, pitch, amplitu...  57.4 us
    pallas_call x1, Pallas kernels, on_device(): pl.pallas_call(functools.partial(scale, ng, nt), out_shape=(jax.ShapeDtyp...  2.75 us

profile of v3, /device:TPU:0, one launch (start us, length us, event | category | flops | bytes accessed | tf_op | source)
XLA Modules:
  0.0 60.8 jit_solution(8692208354290593861)
XLA Ops:
  0.6 57.4 %shard_map.50 = (f32[16,8,8192]{2,1,0:T(8,128)S(1)}, f32[1,128]{1,0:T(1,128)S(1)}) custom-call(s32[64]{0:T(128)} %idx_hbm.1, f32[64,128,128]{2,1,0:T(8,128)} %bitcast.6, f32[4,8,8192]{2,1,0:T(8,128)} %cot_ref.1), custom_call_target="tpu_custom_call" | custom-call | tf_op jit(solution)/shard_map/pallas_call | solution.py:348
  58.1 2.7 %shard_map.51 = (f32[16,8,8192]{2,1,0:T(8,128)}, f32[1,16]{1,0:T(1,128)}) custom-call(f32[16,8,8192]{2,1,0:T(8,128)S(1)} %get-tuple-element.6.d_ref, f32[1,128]{1,0:T(1,128)S(1)} %get-tuple-element.7.n_ref), custom_call_target="tpu_custom_call" | custom-call | tf_op jit(solution)/shard_map/pallas_call | solution.py:383
